TPU v7x, 32 devices: a whole 2x2x4 slice. The times are simulated.
32 devices in a mesh: shot: 4 (over y, core), tile: 8 (over z, x).
Axes of the slice: x: 2, y: 2, z: 4, core: 2. Of those that a mesh axis runs over, the one named last changes fastest.
Arguments:
- source: bfloat16 [64, 1, 32, 32, 128], P(('shot', 'tile')), may hold values from -6 to 6
- receiver: bfloat16 [64, 1, 32, 32, 128], P(('shot', 'tile')), may hold values from -6 to 6
- corners: int32 [64, 2], P(('shot', 'tile')), may hold values from 0 to 224, as said below
Outputs:
- filtered: float32 [32, 256, 256], P('tile', 'shot')
Inputs may be any that keep to these rules, and one draw needn't show every extreme that they name: corners[s, 0] is at most 224 and corners[s, 1] at most 128, so every box lies inside the image.
All inputs are finite; a program needn't handle non-finite values.
Results may differ from a plain program's by a relative error of at most 0.0003.
Values may be sent and summed in bfloat16 or wider, within the bound.
A program may use at most 64 MiB of HBM per device.

v0:
```python
import jax
import jax.numpy as jnp
from jax import lax
from jax.sharding import PartitionSpec as P

X = 256
Y = 256
damping = 1.0


def with_halo(cells, sides, width):
    for axis, dim in sides:
        count = lax.axis_size(axis)
        ends = count - 1
        head = lax.slice_in_dim(cells, 0, width, axis=dim)
        tail = lax.slice_in_dim(cells, cells.shape[dim] - width, cells.shape[dim], axis=dim)
        cells = jnp.concatenate(
            [
                lax.ppermute(tail, axis, [(i, (i + 1) % count) for i in range(ends)]),
                cells,
                lax.ppermute(head, axis, [((i + 1) % count, i) for i in range(ends)]),
            ],
            axis=dim,
        )
    return cells


def laplace(padded):
    center = padded[1:-1, 1:-1, 1:-1]
    beside = padded[2:, 1:-1, 1:-1] + padded[:-2, 1:-1, 1:-1]
    beside = beside + padded[1:-1, 2:, 1:-1] + padded[1:-1, :-2, 1:-1]
    beside = beside + padded[1:-1, 1:-1, 2:] + padded[1:-1, 1:-1, :-2]
    return beside - 6.0 * center


def correlate(wave_bf, back_bf, time_axis):
    wave = wave_bf.astype(jnp.float32)
    back = back_bf.astype(jnp.float32)
    return jnp.stack((jnp.sum(wave * back, axis=time_axis), jnp.sum(wave * wave, axis=time_axis)))


def per_device(source, receiver, corners):
    tile_count = lax.axis_size("tile")
    slab_depth = source.shape[2] // tile_count
    box_rows = source.shape[3]
    box_cols = source.shape[4]
    got_wave, got_back = (
        lax.all_to_all(source, "tile", split_axis=2, concat_axis=0, tiled=True),
        lax.all_to_all(receiver, "tile", split_axis=2, concat_axis=0, tiled=True),
    )
    stacked = correlate(got_wave, got_back, 1)
    corner_all = lax.all_gather(corners, "tile", axis=0, tiled=True)
    col_index = jnp.arange(Y, dtype=jnp.int32)
    box_col = jnp.arange(box_cols, dtype=jnp.int32)
    col_table = (
        col_index[None, None, :] == corner_all[:, 1][:, None, None] + box_col[None, :, None]
    ).astype(jnp.float32)
    placed = jnp.einsum("qkzab,kby->qzkay", stacked, col_table, precision=lax.Precision.HIGHEST)
    shots_in = corner_all.shape[0]
    placed = placed.reshape(2, slab_depth, shots_in * box_rows, Y)
    row_target = (
        corner_all[:, 0][:, None] + jnp.arange(box_rows, dtype=jnp.int32)[None, :]
    ).reshape(-1)
    row_index = jnp.arange(X, dtype=jnp.int32)
    row_table = (row_target[:, None] == row_index[None, :]).astype(jnp.float32)
    sums = jnp.einsum("rx,qzry->qzxy", row_table, placed, precision=lax.Precision.HIGHEST)
    image_part = sums[0]
    light_part = sums[1]
    image_sum, light_sum = (
        lax.psum_scatter(image_part, "shot", scatter_dimension=1, tiled=True),
        lax.psum_scatter(light_part, "shot", scatter_dimension=1, tiled=True),
    )
    normal = image_sum / (damping + light_sum)
    padded = with_halo(normal, (("shot", 1), ("tile", 0)), 1)
    padded = jnp.pad(padded, ((0, 0), (0, 0), (1, 1)))
    return laplace(padded)


def solution(mesh):
    return jax.shard_map(
        per_device,
        mesh=mesh,
        in_specs=(
            P(("shot", "tile"), None, None, None, None),
            P(("shot", "tile"), None, None, None, None),
            P(("shot", "tile"), None),
        ),
        out_specs=P("tile", "shot", None),
        check_vma=False,
    )
```

profile of v0, /device:TPU:3, one launch (start us, length us, event | category | flops | bytes accessed | tf_op | source)
XLA Modules:
  0.0 143.1 jit_solution(10602599561009317554)
XLA Ops:
  6.5 0.0 copy-start
  6.5 0.0 copy-start.1
  6.5 2.0 %copy.15 = bf16[2,1,32,32,128]{4,3,1,0,2:T(8,128)(2,1)} copy(bf16[2,1,32,32,128]{4,3,2,1,0:T(8,128)(2,1)} %param.3) | data formatting | bytes 1048576 | tf_op args[0]
  8.5 5.8 %all-to-all-start = ((bf16[2,1,32,32,128]{4,3,1,0,2:T(8,128)(2,1)}), bf16[2,1,32,32,128]{4,3,1,0,2:T(8,128)(2,1)S(1)}, u32[]{:S(2)}, u32[]{:S(2)}) async-start(bf16[2,1,32,32,128]{4,3,1,0,2:T(8,128)(2,1)} %copy.15), calls=%async_computation | async-start | bytes 1048576 | tf_op jit(solution)/shard_map/all_to_all | solution.py:48
  14.3 0.0 copy-done
  14.3 0.9 copy.16
  15.2 12.9 %all-to-all-done = bf16[2,1,32,32,128]{4,3,1,0,2:T(8,128)(2,1)S(1)} async-done(((bf16[2,1,32,32,128]{4,3,1,0,2:T(8,128)(2,1)}), bf16[2,1,32,32,128]{4,3,1,0,2:T(8,128)(2,1)S(1)}, u32[]{:S(2)}, u32[]{:S(2)}) %all-to-all-start) | async-done | bytes 524320 | tf_op jit(solution)/shard_map/all_to_all | solution.py:48
  28.1 4.5 %all-to-all-start.1 = ((bf16[2,1,32,32,128]{4,3,1,0,2:T(8,128)(2,1)}), bf16[2,1,32,32,128]{4,3,1,0,2:T(8,128)(2,1)S(1)}, u32[]{:S(2)}, u32[]{:S(2)}) async-start(bf16[2,1,32,32,128]{4,3,1,0,2:T(8,128)(2,1)} %copy.16), calls=%async_computation.1 | async-start | bytes 1048576 | tf_op jit(solution)/shard_map/all_to_all | solution.py:49
  32.6 0.0 all-reduce.6.cloned.1.call-start
  32.6 0.0 copy-done.1
  32.6 19.9 %all-gather = s32[8,2,2]{2,1,0:T(2,128)S(1)} all-gather(s32[1,2,2]{2,1,0:T(2,128)S(1)} %bitcast.41), channel_id=1, replica_groups=mesh['shot'=4,'tile'=8] {'tile'}, dimensions={0}, use_global_device_ids=true | all-gather | bytes 144 | tf_op jit(solution)/shard_map/all_gather | solution.py:52
  52.5 0.1 fusion.17
  52.6 0.1 copy.29
  52.7 0.1 copy.28
  52.7 0.1 iota_add_fusion
  52.8 0.1 add.74
  52.9 0.1 iota_add_fusion.1
  53.0 0.0 all-to-all-done.1
  53.0 0.3 convert_multiply_fusion.1
  53.3 0.1 copy.17
  53.4 0.1 copy.18
  53.4 2.3 %convolution_bitcast_fusion = f32[2,4,16,32,256]{4,3,1,0,2:T(8,128)S(1)} fusion(f32[1,16,4,32,128]{4,3,2,0,1:T(8,128)S(1)} %bitcast.37, f32[1,16,4,32,128]{4,3,2,0,1:T(8,128)S(1)} %bitcast.36, s32[16,128]{1,0:T(8,128)S(1)} %iota_add_fusion.1), kind=kOutput, calls=%fused_computation | convolution fusion | flops 1611661312 | bytes 6299648 | tf_op jit(solution)/shard_map/qkzab,kby->qzkay/dot_general | solution.py:58
  55.7 0.6 copy.19
  56.3 3.6 %convolution_bitcast_fusion.1 = f32[2,4,256,256]{2,3,1,0:T(8,128)S(1)} fusion(f32[2,4,512,256]{3,2,1,0:T(8,128)S(1)} %bitcast.33, s32[512]{0:T(512)S(1)} %add.74), kind=kOutput, calls=%fused_computation.6 | convolution fusion | flops 3221356544 | bytes 6293504 | tf_op jit(solution)/shard_map/rx,qzry->qzxy/dot_general | solution.py:66
  60.0 0.2 slice_bitcast_fusion.1
  60.2 1.3 copy.21
  61.5 0.0 copy-start.2
  61.5 1.3 copy.22
  62.8 0.0 all-reduce.6.cloned.1.call-update
  62.9 0.0 copy-done.2
  62.9 0.6 dynamic-slice
  64.1 51.9 %all-reduce.6.cloned.1.call-done = (f32[4,256,256]{2,0,1:T(4,128)}, f32[4,256,256]{2,0,1:T(4,128)}) async-done(((f32[4,256,256]{2,0,1:T(4,128)}, f32[4,256,256]{2,0,1:T(4,128)}), (f32[4,256,256]{2,0,1:T(4,128)}, f32[4,256,256]{2,0,1:T(4,128)})) %all-reduce.6.cloned.1.call-update) | async-done | bytes 2097168
  116.0 1.1 fusion.13
  117.1 3.1 %collective-permute-start = (f32[4,1,256]{2,0,1:T(4,128)S(1)}, f32[4,1,256]{2,0,1:T(4,128)S(1)}, u32[]{:S(2)}, u32[]{:S(2)}) collective-permute-start(f32[4,1,256]{2,0,1:T(4,128)S(1)} %get-tuple-element.13), channel_id=1, source_target_pairs={{0,8},{8,16},{16,24},{1,9},{9,17},{17,25},{2,10},{10,18},{18,26},{... | collective-permute-start | bytes 12296 | tf_op jit(solution)/shard_map/ppermute | solution.py:19
  120.2 1.9 %collective-permute-start.1 = (f32[4,1,256]{2,0,1:T(4,128)S(1)}, f32[4,1,256]{2,0,1:T(4,128)S(1)}, u32[]{:S(2)}, u32[]{:S(2)}) collective-permute-start(f32[4,1,256]{2,0,1:T(4,128)S(1)} %get-tuple-element.14), channel_id=1, source_target_pairs={{8,0},{16,8},{24,16},{9,1},{17,9},{25,17},{10,2},{18,10},{26,18},{... | collective-permute-start | bytes 12296 | tf_op jit(solution)/shard_map/ppermute | solution.py:21
  122.1 0.0 collective-permute-done
  122.1 3.0 %collective-permute-done.1 = f32[4,1,256]{2,0,1:T(4,128)S(1)} collective-permute-done((f32[4,1,256]{2,0,1:T(4,128)S(1)}, f32[4,1,256]{2,0,1:T(4,128)S(1)}, u32[]{:S(2)}, u32[]{:S(2)}) %collective-permute-start.1) | collective-permute-done | bytes 4128 | tf_op jit(solution)/shard_map/ppermute | solution.py:21
  125.1 0.1 pad_maximum_fusion.8
  125.2 3.1 %collective-permute-start.3 = (f32[1,66,256]{2,0,1:T(1,128)S(1)}, f32[1,66,256]{2,0,1:T(1,128)S(1)}, u32[]{:S(2)}, u32[]{:S(2)}) collective-permute-start(f32[1,66,256]{2,0,1:T(1,128)S(1)} %get-tuple-element.11), channel_id=1, source_target_pairs={{0,1},{1,2},{2,3},{3,4},{4,5},{5,6},{6,7},{8,9},{9,10},{10,11},{11... | collective-permute-start | bytes 202760 | tf_op jit(solution)/shard_map/ppermute | solution.py:19
  128.3 2.2 %collective-permute-start.2 = (f32[1,66,256]{2,0,1:T(1,128)S(1)}, f32[1,66,256]{2,0,1:T(1,128)S(1)}, u32[]{:S(2)}, u32[]{:S(2)}) collective-permute-start(f32[1,66,256]{2,0,1:T(1,128)S(1)} %get-tuple-element.12), channel_id=1, source_target_pairs={{1,0},{2,1},{3,2},{4,3},{5,4},{6,5},{7,6},{9,8},{10,9},{11,10},{12... | collective-permute-start | bytes 202760 | tf_op jit(solution)/shard_map/ppermute | solution.py:21
  130.5 0.0 collective-permute-done.3
  130.5 3.7 %collective-permute-done.2 = f32[1,66,256]{2,0,1:T(1,128)S(1)} collective-permute-done((f32[1,66,256]{2,0,1:T(1,128)S(1)}, f32[1,66,256]{2,0,1:T(1,128)S(1)}, u32[]{:S(2)}, u32[]{:S(2)}) %collective-permute-start.2) | collective-permute-done | bytes 67616 | tf_op jit(solution)/shard_map/ppermute | solution.py:21
  134.3 0.7 select_maximum_fusion
  135.0 0.5 fusion.9
  135.5 0.8 copy.23
  (1 shorter events, 0.0 us)
Async XLA Ops:
  6.5 7.8 %copy-start = (bf16[2,1,32,32,128]{4,3,2,1,0:T(8,128)(2,1)S(1)}, bf16[2,1,32,32,128]{4,3,2,1,0:T(8,128)(2,1)}, u32[]{:S(2)}) copy-start(bf16[2,1,32,32,128]{4,3,2,1,0:T(8,128)(2,1)} %param.4) | copy-start | bytes 1572868
  6.5 26.1 %copy-start.1 = (s32[2,2]{1,0:T(2,128)S(1)}, s32[2,2]{1,0:T(2,128)}, u32[]{:S(2)}) copy-start(s32[2,2]{1,0:T(2,128)} %param.5) | copy-start | bytes 52
  8.5 19.5 %all-to-all-start = ((bf16[2,1,32,32,128]{4,3,1,0,2:T(8,128)(2,1)}), bf16[2,1,32,32,128]{4,3,1,0,2:T(8,128)(2,1)S(1)}, u32[]{:S(2)}, u32[]{:S(2)}) async-start(bf16[2,1,32,32,128]{4,3,1,0,2:T(8,128)(2,1)} %copy.15), calls=%async_computation | async-start | bytes 1048576 | tf_op jit(solution)/shard_map/all_to_all | solution.py:48
  28.1 24.9 %all-to-all-start.1 = ((bf16[2,1,32,32,128]{4,3,1,0,2:T(8,128)(2,1)}), bf16[2,1,32,32,128]{4,3,1,0,2:T(8,128)(2,1)S(1)}, u32[]{:S(2)}, u32[]{:S(2)}) async-start(bf16[2,1,32,32,128]{4,3,1,0,2:T(8,128)(2,1)} %copy.16), calls=%async_computation.1 | async-start | bytes 1048576 | tf_op jit(solution)/shard_map/all_to_all | solution.py:49
  32.6 83.4 %all-reduce.6.cloned.1.call-start = ((), (), s32[]{:S(2)}) async-start(), calls=%async_computation.2 | async-start | bytes 4194304
  61.5 1.3 copy-start.2
  117.1 5.0 %collective-permute-start = (f32[4,1,256]{2,0,1:T(4,128)S(1)}, f32[4,1,256]{2,0,1:T(4,128)S(1)}, u32[]{:S(2)}, u32[]{:S(2)}) collective-permute-start(f32[4,1,256]{2,0,1:T(4,128)S(1)} %get-tuple-element.13), channel_id=1, source_target_pairs={{0,8},{8,16},{16,24},{1,9},{9,17},{17,25},{2,10},{10,18},{18,26},{... | collective-permute-start | bytes 12296 | tf_op jit(solution)/shard_map/ppermute | solution.py:19
  120.2 4.9 %collective-permute-start.1 = (f32[4,1,256]{2,0,1:T(4,128)S(1)}, f32[4,1,256]{2,0,1:T(4,128)S(1)}, u32[]{:S(2)}, u32[]{:S(2)}) collective-permute-start(f32[4,1,256]{2,0,1:T(4,128)S(1)} %get-tuple-element.14), channel_id=1, source_target_pairs={{8,0},{16,8},{24,16},{9,1},{17,9},{25,17},{10,2},{18,10},{26,18},{... | collective-permute-start | bytes 12296 | tf_op jit(solution)/shard_map/ppermute | solution.py:21
  125.2 5.3 %collective-permute-start.3 = (f32[1,66,256]{2,0,1:T(1,128)S(1)}, f32[1,66,256]{2,0,1:T(1,128)S(1)}, u32[]{:S(2)}, u32[]{:S(2)}) collective-permute-start(f32[1,66,256]{2,0,1:T(1,128)S(1)} %get-tuple-element.11), channel_id=1, source_target_pairs={{0,1},{1,2},{2,3},{3,4},{4,5},{5,6},{6,7},{8,9},{9,10},{10,11},{11... | collective-permute-start | bytes 202760 | tf_op jit(solution)/shard_map/ppermute | solution.py:19
  128.3 5.9 %collective-permute-start.2 = (f32[1,66,256]{2,0,1:T(1,128)S(1)}, f32[1,66,256]{2,0,1:T(1,128)S(1)}, u32[]{:S(2)}, u32[]{:S(2)}) collective-permute-start(f32[1,66,256]{2,0,1:T(1,128)S(1)} %get-tuple-element.12), channel_id=1, source_target_pairs={{1,0},{2,1},{3,2},{4,3},{5,4},{6,5},{7,6},{9,8},{10,9},{11,10},{12... | collective-permute-start | bytes 202760 | tf_op jit(solution)/shard_map/ppermute | solution.py:21
Sparse Core Ops, SparseCore 0:
  63.0 52.9 all-reduce.5
where the time goes:
time: 143 us
  waiting for transfers between devices  71.5 us (50%)
  starting transfers between devices  20.6 us (14%)
  blocking collectives  19.9 us (14%)
  between operations  14.2 us (10%)
  local copies, waits for them, and re-layouts  8.1 us (6%)
  matrix products  5.91 us (4%)
  other arithmetic  2.88 us (2%)
    unnamed x2, waiting for transfers between devices  51.9 us
    all_gather x1, blocking collectives, per_device(): corner_all = lax.all_gather(corners, 'tile', axis=0, tiled=True)  19.9 us
    all_to_all x1, waiting for transfers between devices, per_device(): lax.all_to_all(source, 'tile', split_axis=2, concat_axis=0, tiled=True)  12.9 us
    ppermute x2, waiting for transfers between devices, with_halo(): lax.ppermute(head, axis, [((i + 1) % count, i) for i in range(ends)])  6.73 us
    ppermute x2, starting transfers between devices, with_halo(): lax.ppermute(tail, axis, [(i, (i + 1) % count) for i in range(ends)])  6.16 us
    all_to_all x1, starting transfers between devices, per_device(): lax.all_to_all(source, 'tile', split_axis=2, concat_axis=0, tiled=True)  5.78 us
    all_to_all x1, starting transfers between devices, per_device(): lax.all_to_all(receiver, 'tile', split_axis=2, concat_axis=0, tiled=True)  4.54 us
    ppermute x2, starting transfers between devices, with_halo(): lax.ppermute(head, axis, [((i + 1) % count, i) for i in range(ends)])  4.09 us
  transfers between devices with their start and end apart: 7, of which 4 were waited for; matrix products, arithmetic and copies ran while one was open for 1% of the time, Pallas kernels for 0%

commit v1 on v0

--- a/solution.py
+++ b/solution.py
@@ -49,7 +49,16 @@
         lax.all_to_all(receiver, "tile", split_axis=2, concat_axis=0, tiled=True),
     )
     stacked = correlate(got_wave, got_back, 1)
-    corner_all = lax.all_gather(corners, "tile", axis=0, tiled=True)
+    x_now = lax.psum(1, axis_name="tile")
+    shaped = lax.axis_index("tile")
+    z1, arr_now, tile_out = (x_now, shaped, corners.shape[0])
+    reply, m_next = (corners, 1)
+    while m_next < z1:
+        left_arr = tuple(((d, (d - m_next) % z1) for d in range(z1)))
+        y = lax.ppermute(reply, axis_name="tile", perm=left_arr)
+        reply = jnp.concatenate([reply, y], 0)
+        m_next = 2 * m_next
+    corner_all = jnp.roll(reply, arr_now * tile_out, 0)
     col_index = jnp.arange(Y, dtype=jnp.int32)
     box_col = jnp.arange(box_cols, dtype=jnp.int32)
     col_table = (

time: 143 us -> 139 us (0.972); the launches traced: 143 us -> 137 us
  blocking collectives: 19.9 us -> 0 us
  starting transfers between devices: 20.6 us -> 29.5 us
  waiting for transfers between devices: 71.5 us -> 76.2 us
    all_gather x1 -> x0, blocking collectives: 19.9 us -> none  [per_device(): corner_all = lax.all_gather(corners, 'tile', axis=0, tiled=True)]
    ppermute x0 -> x3, starting transfers between devices: none -> 8.06 us  [per_device(): y = lax.ppermute(reply, axis_name='tile', perm=left_arr)]
    ppermute x0 -> x3, waiting for transfers between devices: none -> 6.27 us  [per_device(): y = lax.ppermute(reply, axis_name='tile', perm=left_arr)]
    ppermute x2, waiting for transfers between devices: 6.73 us -> 2.99 us  [with_halo(): lax.ppermute(head, axis, [((i + 1) % count, i) for i in range(ends)])]
    unnamed x11 -> x10, local copies, waits for them, and re-layouts: 3.6 us -> 3.52 us
  transfers between devices with their start and end apart: 7 -> 10, of which waited for: 4 -> 6; matrix products, arithmetic and copies ran while one was open for 1% -> 2% of each run, Pallas kernels for 0% -> 0%
where the time goes in v1:
time: 139 us; the launch traced here: 137 us
  waiting for transfers between devices  76.2 us (55%)
  starting transfers between devices  29.5 us (21%)
  between operations  14.2 us (10%)
  local copies, waits for them, and re-layouts  8.1 us (6%)
  matrix products  5.9 us (4%)
  other arithmetic  3.03 us (2%)
    unnamed x2, waiting for transfers between devices  52.9 us
    all_to_all x1, waiting for transfers between devices, per_device(): lax.all_to_all(source, 'tile', split_axis=2, concat_axis=0, tiled=True)  12.8 us
    ppermute x3, starting transfers between devices, per_device(): y = lax.ppermute(reply, axis_name='tile', perm=left_arr)  8.06 us
    ppermute x2, starting transfers between devices, with_halo(): lax.ppermute(tail, axis, [(i, (i + 1) % count) for i in range(ends)])  7.25 us
    ppermute x3, waiting for transfers between devices, per_device(): y = lax.ppermute(reply, axis_name='tile', perm=left_arr)  6.27 us
    all_to_all x1, starting transfers between devices, per_device(): lax.all_to_all(source, 'tile', split_axis=2, concat_axis=0, tiled=True)  5.78 us
    all_to_all x1, starting transfers between devices, per_device(): lax.all_to_all(receiver, 'tile', split_axis=2, concat_axis=0, tiled=True)  4.54 us
    ppermute x2, starting transfers between devices, with_halo(): lax.ppermute(head, axis, [((i + 1) % count, i) for i in range(ends)])  3.9 us
  transfers between devices with their start and end apart: 10, of which 6 were waited for; matrix products, arithmetic and copies ran while one was open for 2% of the time, Pallas kernels for 0%

profile of v1, /device:TPU:3, one launch (start us, length us, event | category | flops | bytes accessed | tf_op | source)
XLA Modules:
  0.0 137.0 jit_solution(15454894999807488901)
XLA Ops:
  6.5 0.0 copy-start.1
  6.5 0.0 copy-start
  6.5 2.0 %copy.17 = bf16[2,1,32,32,128]{4,3,1,0,2:T(8,128)(2,1)} copy(bf16[2,1,32,32,128]{4,3,2,1,0:T(8,128)(2,1)} %param.3) | data formatting | bytes 1048576 | tf_op args[0]
  8.5 5.8 %all-to-all-start = ((bf16[2,1,32,32,128]{4,3,1,0,2:T(8,128)(2,1)}), bf16[2,1,32,32,128]{4,3,1,0,2:T(8,128)(2,1)S(1)}, u32[]{:S(2)}, u32[]{:S(2)}) async-start(bf16[2,1,32,32,128]{4,3,1,0,2:T(8,128)(2,1)} %copy.17), calls=%async_computation | async-start | bytes 1048576 | tf_op jit(solution)/shard_map/all_to_all | solution.py:48
  14.3 0.0 copy-done.1
  14.3 0.1 copy.15
  14.4 0.0 collective-permute-start
  14.4 0.0 copy-done
  14.4 0.9 copy.18
  15.3 12.8 %all-to-all-done = bf16[2,1,32,32,128]{4,3,1,0,2:T(8,128)(2,1)S(1)} async-done(((bf16[2,1,32,32,128]{4,3,1,0,2:T(8,128)(2,1)}), bf16[2,1,32,32,128]{4,3,1,0,2:T(8,128)(2,1)S(1)}, u32[]{:S(2)}, u32[]{:S(2)}) %all-to-all-start) | async-done | bytes 524320 | tf_op jit(solution)/shard_map/all_to_all | solution.py:48
  28.1 4.5 %all-to-all-start.1 = ((bf16[2,1,32,32,128]{4,3,1,0,2:T(8,128)(2,1)}), bf16[2,1,32,32,128]{4,3,1,0,2:T(8,128)(2,1)S(1)}, u32[]{:S(2)}, u32[]{:S(2)}) async-start(bf16[2,1,32,32,128]{4,3,1,0,2:T(8,128)(2,1)} %copy.18), calls=%async_computation.1 | async-start | bytes 1048576 | tf_op jit(solution)/shard_map/all_to_all | solution.py:49
  32.6 0.0 all-reduce.6.cloned.1.call-start
  32.6 0.0 collective-permute-done
  32.6 0.1 pad_add_fusion
  32.7 3.0 %collective-permute-start.1 = (s32[4,2]{0,1:T(2,128)S(1)}, s32[4,2]{0,1:T(2,128)S(1)}, u32[]{:S(2)}, u32[]{:S(2)}) collective-permute-start(s32[4,2]{0,1:T(2,128)S(1)} %pad_add_fusion), channel_id=1, source_target_pairs={{0,6},{1,7},{2,0},{3,1},{4,2},{5,3},{6,4},{7,5},{8,14},{9,15},{10,... | collective-permute-start | bytes 104 | tf_op jit(solution)/shard_map/ppermute | solution.py:58
  35.7 5.0 %collective-permute-done.1 = s32[4,2]{0,1:T(2,128)S(1)} collective-permute-done((s32[4,2]{0,1:T(2,128)S(1)}, s32[4,2]{0,1:T(2,128)S(1)}, u32[]{:S(2)}, u32[]{:S(2)}) %collective-permute-start.1) | collective-permute-done | bytes 64 | tf_op jit(solution)/shard_map/ppermute | solution.py:58
  40.7 0.1 pad_add_fusion.1
  40.7 5.1 %collective-permute-start.2 = (s32[8,2]{0,1:T(2,128)S(1)}, s32[8,2]{0,1:T(2,128)S(1)}, u32[]{:S(2)}, u32[]{:S(2)}) collective-permute-start(s32[8,2]{0,1:T(2,128)S(1)} %pad_add_fusion.1), channel_id=1, source_target_pairs={{0,4},{1,5},{2,6},{3,7},{4,0},{5,1},{6,2},{7,3},{8,12},{9,13},{10,... | collective-permute-start | bytes 200 | tf_op jit(solution)/shard_map/ppermute | solution.py:58
  45.8 1.3 collective-permute-done.2
  47.1 0.1 concatenate.34
  47.2 0.1 constant_dynamic-slice_fusion
  47.3 0.1 iota_add_fusion
  47.3 0.1 add.86
  47.4 0.1 iota_add_fusion.1
  47.5 0.0 all-to-all-done.1
  47.5 0.3 convert_multiply_fusion.1
  47.8 0.1 copy.19
  47.9 0.1 copy.20
  48.0 2.3 %convolution_bitcast_fusion = f32[2,4,16,32,256]{4,3,1,0,2:T(8,128)S(1)} fusion(f32[1,16,4,32,128]{4,3,2,0,1:T(8,128)S(1)} %bitcast.37, f32[1,16,4,32,128]{4,3,2,0,1:T(8,128)S(1)} %bitcast.36, s32[16,128]{1,0:T(8,128)S(1)} %iota_add_fusion.1), kind=kOutput, calls=%fused_computation | convolution fusion | flops 1611661312 | bytes 6299648 | tf_op jit(solution)/shard_map/qkzab,kby->qzkay/dot_general | solution.py:67
  50.2 0.6 copy.21
  50.8 3.6 %convolution_bitcast_fusion.1 = f32[2,4,256,256]{2,3,1,0:T(8,128)S(1)} fusion(f32[2,4,512,256]{3,2,1,0:T(8,128)S(1)} %bitcast.33, s32[512]{0:T(512)S(1)} %add.86), kind=kOutput, calls=%fused_computation.6 | convolution fusion | flops 3221356544 | bytes 6293504 | tf_op jit(solution)/shard_map/rx,qzry->qzxy/dot_general | solution.py:75
  54.5 0.2 slice_bitcast_fusion.1
  54.7 1.3 copy.23
  56.0 0.0 copy-start.2
  56.0 1.3 copy.24
  57.3 0.0 all-reduce.6.cloned.1.call-update
  57.3 0.0 copy-done.2
  57.4 0.6 dynamic-slice
  58.6 52.8 %all-reduce.6.cloned.1.call-done = (f32[4,256,256]{2,0,1:T(4,128)}, f32[4,256,256]{2,0,1:T(4,128)}) async-done(((f32[4,256,256]{2,0,1:T(4,128)}, f32[4,256,256]{2,0,1:T(4,128)}), (f32[4,256,256]{2,0,1:T(4,128)}, f32[4,256,256]{2,0,1:T(4,128)})) %all-reduce.6.cloned.1.call-update) | async-done | bytes 2097168
  111.4 1.1 fusion.13
  112.6 3.1 %collective-permute-start.3 = (f32[4,1,256]{2,0,1:T(4,128)S(1)}, f32[4,1,256]{2,0,1:T(4,128)S(1)}, u32[]{:S(2)}, u32[]{:S(2)}) collective-permute-start(f32[4,1,256]{2,0,1:T(4,128)S(1)} %get-tuple-element.13), channel_id=1, source_target_pairs={{0,8},{8,16},{16,24},{1,9},{9,17},{17,25},{2,10},{10,18},{18,26},{... | collective-permute-start | bytes 12296 | tf_op jit(solution)/shard_map/ppermute | solution.py:19
  115.6 1.9 %collective-permute-start.4 = (f32[4,1,256]{2,0,1:T(4,128)S(1)}, f32[4,1,256]{2,0,1:T(4,128)S(1)}, u32[]{:S(2)}, u32[]{:S(2)}) collective-permute-start(f32[4,1,256]{2,0,1:T(4,128)S(1)} %get-tuple-element.14), channel_id=1, source_target_pairs={{8,0},{16,8},{24,16},{9,1},{17,9},{25,17},{10,2},{18,10},{26,18},{... | collective-permute-start | bytes 12296 | tf_op jit(solution)/shard_map/ppermute | solution.py:21
  117.6 0.0 collective-permute-done.3
  117.6 3.0 %collective-permute-done.4 = f32[4,1,256]{2,0,1:T(4,128)S(1)} collective-permute-done((f32[4,1,256]{2,0,1:T(4,128)S(1)}, f32[4,1,256]{2,0,1:T(4,128)S(1)}, u32[]{:S(2)}, u32[]{:S(2)}) %collective-permute-start.4) | collective-permute-done | bytes 4128 | tf_op jit(solution)/shard_map/ppermute | solution.py:21
  120.6 0.1 pad_maximum_fusion.8
  120.7 2.0 %collective-permute-start.5 = (f32[1,66,256]{2,0,1:T(1,128)S(1)}, f32[1,66,256]{2,0,1:T(1,128)S(1)}, u32[]{:S(2)}, u32[]{:S(2)}) collective-permute-start(f32[1,66,256]{2,0,1:T(1,128)S(1)} %get-tuple-element.12), channel_id=1, source_target_pairs={{1,0},{2,1},{3,2},{4,3},{5,4},{6,5},{7,6},{9,8},{10,9},{11,10},{12... | collective-permute-start | bytes 202760 | tf_op jit(solution)/shard_map/ppermute | solution.py:21
  122.7 4.2 %collective-permute-start.6 = (f32[1,66,256]{2,0,1:T(1,128)S(1)}, f32[1,66,256]{2,0,1:T(1,128)S(1)}, u32[]{:S(2)}, u32[]{:S(2)}) collective-permute-start(f32[1,66,256]{2,0,1:T(1,128)S(1)} %get-tuple-element.11), channel_id=1, source_target_pairs={{0,1},{1,2},{2,3},{3,4},{4,5},{5,6},{6,7},{8,9},{9,10},{10,11},{11... | collective-permute-start | bytes 202760 | tf_op jit(solution)/shard_map/ppermute | solution.py:19
  126.9 0.0 collective-permute-done.5
  126.9 1.3 collective-permute-done.6
  128.2 0.7 select_maximum_fusion
  129.0 0.5 fusion.9
  129.4 0.8 copy.25
  (2 shorter events, 0.0 us)
Async XLA Ops:
  6.5 7.8 %copy-start.1 = (s32[2,2]{1,0:T(2,128)S(1)}, s32[2,2]{1,0:T(2,128)}, u32[]{:S(2)}) copy-start(s32[2,2]{1,0:T(2,128)} %param.5) | copy-start | bytes 52
  6.5 7.9 %copy-start = (bf16[2,1,32,32,128]{4,3,2,1,0:T(8,128)(2,1)S(1)}, bf16[2,1,32,32,128]{4,3,2,1,0:T(8,128)(2,1)}, u32[]{:S(2)}) copy-start(bf16[2,1,32,32,128]{4,3,2,1,0:T(8,128)(2,1)} %param.4) | copy-start | bytes 1572868
  8.5 19.5 %all-to-all-start = ((bf16[2,1,32,32,128]{4,3,1,0,2:T(8,128)(2,1)}), bf16[2,1,32,32,128]{4,3,1,0,2:T(8,128)(2,1)S(1)}, u32[]{:S(2)}, u32[]{:S(2)}) async-start(bf16[2,1,32,32,128]{4,3,1,0,2:T(8,128)(2,1)} %copy.17), calls=%async_computation | async-start | bytes 1048576 | tf_op jit(solution)/shard_map/all_to_all | solution.py:48
  14.4 18.2 %collective-permute-start = (s32[2,2]{0,1:T(2,128)S(1)}, s32[2,2]{0,1:T(2,128)S(1)}, u32[]{:S(2)}, u32[]{:S(2)}) collective-permute-start(s32[2,2]{0,1:T(2,128)S(1)} %copy.15), channel_id=1, source_target_pairs={{0,7},{1,0},{2,1},{3,2},{4,3},{5,4},{6,5},{7,6},{8,15},{9,8},{10,9... | collective-permute-start | bytes 56 | tf_op jit(solution)/shard_map/ppermute | solution.py:58
  28.1 19.4 %all-to-all-start.1 = ((bf16[2,1,32,32,128]{4,3,1,0,2:T(8,128)(2,1)}), bf16[2,1,32,32,128]{4,3,1,0,2:T(8,128)(2,1)S(1)}, u32[]{:S(2)}, u32[]{:S(2)}) async-start(bf16[2,1,32,32,128]{4,3,1,0,2:T(8,128)(2,1)} %copy.18), calls=%async_computation.1 | async-start | bytes 1048576 | tf_op jit(solution)/shard_map/all_to_all | solution.py:49
  32.6 78.8 %all-reduce.6.cloned.1.call-start = ((), (), s32[]{:S(2)}) async-start(), calls=%async_computation.2 | async-start | bytes 4194304
  32.7 8.0 %collective-permute-start.1 = (s32[4,2]{0,1:T(2,128)S(1)}, s32[4,2]{0,1:T(2,128)S(1)}, u32[]{:S(2)}, u32[]{:S(2)}) collective-permute-start(s32[4,2]{0,1:T(2,128)S(1)} %pad_add_fusion), channel_id=1, source_target_pairs={{0,6},{1,7},{2,0},{3,1},{4,2},{5,3},{6,4},{7,5},{8,14},{9,15},{10,... | collective-permute-start | bytes 104 | tf_op jit(solution)/shard_map/ppermute | solution.py:58
  40.7 6.3 %collective-permute-start.2 = (s32[8,2]{0,1:T(2,128)S(1)}, s32[8,2]{0,1:T(2,128)S(1)}, u32[]{:S(2)}, u32[]{:S(2)}) collective-permute-start(s32[8,2]{0,1:T(2,128)S(1)} %pad_add_fusion.1), channel_id=1, source_target_pairs={{0,4},{1,5},{2,6},{3,7},{4,0},{5,1},{6,2},{7,3},{8,12},{9,13},{10,... | collective-permute-start | bytes 200 | tf_op jit(solution)/shard_map/ppermute | solution.py:58
  56.0 1.3 copy-start.2
  112.6 5.0 %collective-permute-start.3 = (f32[4,1,256]{2,0,1:T(4,128)S(1)}, f32[4,1,256]{2,0,1:T(4,128)S(1)}, u32[]{:S(2)}, u32[]{:S(2)}) collective-permute-start(f32[4,1,256]{2,0,1:T(4,128)S(1)} %get-tuple-element.13), channel_id=1, source_target_pairs={{0,8},{8,16},{16,24},{1,9},{9,17},{17,25},{2,10},{10,18},{18,26},{... | collective-permute-start | bytes 12296 | tf_op jit(solution)/shard_map/ppermute | solution.py:19
  115.6 4.9 %collective-permute-start.4 = (f32[4,1,256]{2,0,1:T(4,128)S(1)}, f32[4,1,256]{2,0,1:T(4,128)S(1)}, u32[]{:S(2)}, u32[]{:S(2)}) collective-permute-start(f32[4,1,256]{2,0,1:T(4,128)S(1)} %get-tuple-element.14), channel_id=1, source_target_pairs={{8,0},{16,8},{24,16},{9,1},{17,9},{25,17},{10,2},{18,10},{26,18},{... | collective-permute-start | bytes 12296 | tf_op jit(solution)/shard_map/ppermute | solution.py:21
  120.7 6.2 %collective-permute-start.5 = (f32[1,66,256]{2,0,1:T(1,128)S(1)}, f32[1,66,256]{2,0,1:T(1,128)S(1)}, u32[]{:S(2)}, u32[]{:S(2)}) collective-permute-start(f32[1,66,256]{2,0,1:T(1,128)S(1)} %get-tuple-element.12), channel_id=1, source_target_pairs={{1,0},{2,1},{3,2},{4,3},{5,4},{6,5},{7,6},{9,8},{10,9},{11,10},{12... | collective-permute-start | bytes 202760 | tf_op jit(solution)/shard_map/ppermute | solution.py:21
  122.7 5.5 %collective-permute-start.6 = (f32[1,66,256]{2,0,1:T(1,128)S(1)}, f32[1,66,256]{2,0,1:T(1,128)S(1)}, u32[]{:S(2)}, u32[]{:S(2)}) collective-permute-start(f32[1,66,256]{2,0,1:T(1,128)S(1)} %get-tuple-element.11), channel_id=1, source_target_pairs={{0,1},{1,2},{2,3},{3,4},{4,5},{5,6},{6,7},{8,9},{9,10},{10,11},{11... | collective-permute-start | bytes 202760 | tf_op jit(solution)/shard_map/ppermute | solution.py:19
Sparse Core Ops, SparseCore 0:
  57.5 53.9 all-reduce.5
